TPU v7x, 32 devices: a whole 2x2x4 slice. The times are simulated.
32 devices in a mesh: gx: 4 (over z), gy: 4 (over y, x), gz: 2 (over core).
Axes of the slice: x: 2, y: 2, z: 4, core: 2. Of those that a mesh axis runs over, the one named last changes fastest.
Arguments:
- pair: bfloat16 [128, 128, 128], P('gx', ('gy', 'gz')), may hold values from -6 to 6
- pair_mask: int32 [128, 128], P('gx', ('gy', 'gz')), may hold values 0 or 1
- in_gain: float32 [128], replicated, may hold values from 0.1 to 1.9
- in_bias: float32 [128], replicated, may hold values from -3 to 3
- proj_weight: bfloat16 [128, 512], replicated, may hold values from -0.5 to 0.5
- gate_weight: bfloat16 [128, 128], replicated, may hold values from -0.5 to 0.5
- out_gain: float32 [128], replicated, may hold values from 0.1 to 1.9
- out_bias: float32 [128], replicated, may hold values from -3 to 3
- out_weight: bfloat16 [128, 128], replicated, may hold values from -0.5 to 0.5
Outputs:
- update: bfloat16 [128, 128, 128], P('gx', ('gy', 'gz'))
All inputs are finite; a program needn't handle non-finite values. No bound on the sum of `pair_mask` on one device may be relied on, other than what follows from the above.
Results may differ from a plain program's by a relative error of at most 0.0071.
Values may be sent and summed in bfloat16 or wider, within the bound.
A program may use at most 64 MiB of HBM per device.

v0:
```python
import jax
import jax.numpy as jnp
from jax import lax
from jax.sharding import PartitionSpec as P


def normalize(values, gain, bias):
    average = jnp.mean(values, axis=-1, keepdims=True)
    centered = values - average
    variance = jnp.mean(centered * centered, axis=-1, keepdims=True)
    return centered * lax.rsqrt(variance + 1e-05) * gain + bias


def project(tile, mask_value, in_gain, in_bias, proj_weight):
    hidden = proj_weight.shape[1] // 4
    normed = normalize(tile.astype(jnp.float32), in_gain, in_bias).astype(jnp.bfloat16)
    projected = jnp.einsum("rwc,cd->rwd", normed, proj_weight, preferred_element_type=jnp.float32)
    left_side = (
        jax.nn.sigmoid(projected[:, :, :hidden]) * projected[:, :, hidden : 2 * hidden] * mask_value
    ).astype(jnp.bfloat16)
    right_side = (
        jax.nn.sigmoid(projected[:, :, 2 * hidden : 3 * hidden])
        * projected[:, :, 3 * hidden :]
        * mask_value
    ).astype(jnp.bfloat16)
    return (normed, left_side, right_side)


def on_device(
    pair, pair_mask, in_gain, in_bias, proj_weight, gate_weight, out_gain, out_bias, out_weight
):
    mask_value = pair_mask.astype(jnp.float32)[:, :, None]
    normed, left_side, own_right = project(pair, mask_value, in_gain, in_bias, proj_weight)
    left_slab, right_slab = (
        lax.all_gather(left_side, "gy", axis=1, tiled=True),
        lax.all_gather(own_right, "gy", axis=1, tiled=True),
    )
    every_row = lax.all_gather(own_right, "gx", axis=0, tiled=True)
    row_panel = lax.all_to_all(every_row, "gy", split_axis=0, concat_axis=1, tiled=True)
    summed = lax.psum_scatter(
        jnp.einsum("jkc,ikc->jic", row_panel, left_slab, preferred_element_type=jnp.float32),
        "gz",
        scatter_dimension=0,
        tiled=True,
    )
    triangle = jnp.transpose(summed, (1, 0, 2))
    tri_normed = normalize(triangle, out_gain, out_bias).astype(jnp.bfloat16)
    gating = jax.nn.sigmoid(
        jnp.einsum("rwc,cd->rwd", normed, gate_weight, preferred_element_type=jnp.float32)
    )
    mixed = jnp.einsum("rwh,hc->rwc", tri_normed, out_weight, preferred_element_type=jnp.float32)
    return (gating * mixed).astype(jnp.bfloat16)


def solution(mesh):
    return jax.shard_map(
        on_device,
        mesh=mesh,
        in_specs=(
            P("gx", ("gy", "gz"), None),
            P("gx", ("gy", "gz")),
            P(),
            P(),
            P(),
            P(),
            P(),
            P(),
            P(),
        ),
        out_specs=P("gx", ("gy", "gz"), None),
        check_vma=False,
    )
```

profile of v0, /device:TPU:0, one launch (start us, length us, event | category | flops | bytes accessed | tf_op | source)
XLA Modules:
  0.0 80.6 jit_solution(6983659560410940790)
XLA Ops:
  6.5 0.0 copy-start
  6.5 1.1 %convert_reduce_fusion = f32[32,16]{1,0:T(8,128)S(1)} fusion(bf16[32,16,128]{2,1,0:T(8,128)(2,1)} %param.9), kind=kLoop, calls=%fused_computation.8 | loop fusion | flops 130560 | bytes 133120 | tf_op jit(solution)/shard_map/reduce_sum | solution.py:8
  7.6 0.1 copy.52
  7.7 0.1 copy.53
  7.8 1.1 %fusion.6 = f32[32,16]{1,0:T(8,128)S(1)} fusion(bf16[32,16,128]{2,1,0:T(8,128)(2,1)} %param.9, f32[32,16]{1,0:T(8,128)S(1)} %copy.53), kind=kLoop, calls=%fused_computation.11 | loop fusion | flops 261632 | bytes 135168 | tf_op jit(solution)/shard_map/reduce_sum | solution.py:10
  8.9 0.1 copy.54
  9.0 0.1 copy.55
  9.1 0.7 convert_element_type.23
  9.8 0.1 copy.56
  9.9 0.0 copy-done
  9.9 1.3 %fusion.20 = f32[32,16,512]{2,1,0:T(8,128)S(1)} fusion(bf16[128,512]{1,0:T(8,128)(2,1)S(1)} %copy-done, bf16[32,16,128]{2,1,0:T(8,128)(2,1)} %param.9, f32[128]{0:T(128)} %param.12, f32[128]{0:T(128)} %param.11, f32[32,16]{1,0:T(8,128)S(1)} %copy.55, f32[32,16]{1,0:T(8,128)S(1)} %copy.53), kind=kOutput, calls=%fused_computation.33 | convolution fusion | flops 67502080 | bytes 1315840 | tf_op jit(solution)/shard_map/rwc,cd->rwd/dot_general | solution.py:17
  11.2 0.2 fusion.11
  11.3 18.0 %all_gather.7 = bf16[128,16,128]{2,1,0:T(8,128)(2,1)} all-gather(bf16[32,16,128]{2,1,0:T(8,128)(2,1)S(1)} %get-tuple-element.5), channel_id=1, replica_groups=mesh['gx'=4,'gy'=4,'gz'=2] {'gx'}, dimensions={0}, use_global_device_ids=true | all-gather | bytes 655360 | tf_op jit(solution)/shard_map/all_gather | solution.py:38
  29.3 3.7 %all-to-all-start = ((bf16[128,16,128]{2,1,0:T(8,128)(2,1)}), bf16[128,16,128]{2,1,0:T(8,128)(2,1)S(1)}, u32[]{:S(2)}, u32[]{:S(2)}) async-start(bf16[128,16,128]{2,1,0:T(8,128)(2,1)} %all_gather.7), calls=%async_computation | async-start | bytes 1048576 | tf_op jit(solution)/shard_map/all_to_all | solution.py:39
  33.1 0.0 reduce-scatter.2.cloned.1.call-start
  33.1 15.6 %all_gather.6 = bf16[32,64,128]{2,1,0:T(8,128)(2,1)S(1)} all-gather(bf16[32,16,128]{2,1,0:T(8,128)(2,1)S(1)} %get-tuple-element.6), channel_id=1, replica_groups=mesh['gx'=4,'gy'=4,'gz'=2] {'gy'}, dimensions={1}, use_global_device_ids=true | all-gather | bytes 655360 | tf_op jit(solution)/shard_map/all_gather | solution.py:35
  48.7 3.2 %copy.58 = bf16[32,64,128]{0,1,2:T(8,128)(2,1)S(1)} copy(bf16[32,64,128]{2,1,0:T(8,128)(2,1)S(1)} %all_gather.6) | data formatting | bytes 1048576 | tf_op jit(solution)/shard_map/all_gather | solution.py:35
  51.9 0.0 all-to-all-done
  51.9 0.9 %copy.57 = bf16[32,4,16,128]{3,2,1,0:T(8,128)(2,1)} copy(bf16[32,4,16,128]{3,2,0,1:T(8,128)(2,1)S(1)} %bitcast.25) | data formatting | bytes 1048576 | tf_op jit(solution)/shard_map/all_to_all | solution.py:39
  52.8 2.5 %copy.59 = bf16[32,64,128]{1,0,2:T(8,128)(2,1)S(1)} copy(bf16[32,64,128]{2,1,0:T(8,128)(2,1)} %bitcast.24) | data formatting | bytes 1048576 | tf_op jit(solution)/shard_map/all_to_all | solution.py:39
  55.2 2.1 %convolution_bitcast_fusion = f32[32,32,128]{0,1,2:T(8,128)} fusion(bf16[32,64,128]{0,1,2:T(8,128)(2,1)S(1)} %copy.58, bf16[32,64,128]{1,0,2:T(8,128)(2,1)S(1)} %copy.59), kind=kOutput, calls=%fused_computation | convolution fusion | flops 16777216 | bytes 1572864 | tf_op jit(solution)/shard_map/jkc,ikc->jic/dot_general | solution.py:41
  57.3 0.0 copy-start.1
  57.3 0.0 copy-start.3
  57.3 0.0 copy-start.4
  57.3 0.0 copy-start.7
  57.3 0.0 copy-start.5
  57.4 0.0 copy-start.6
  57.4 3.7 %copy.60 = f32[32,32,128]{2,1,0:T(8,128)} copy(f32[32,32,128]{0,1,2:T(8,128)} %convolution_bitcast_fusion) | data formatting | bytes 1048576 | tf_op jit(solution)/shard_map/jkc,ikc->jic/transpose | solution.py:41
  61.1 0.0 copy-start.2
  61.1 0.0 reduce-scatter.2.cloned.1.call-update
  61.1 0.0 copy-done.1
  61.1 0.0 copy-done.3
  61.1 0.0 copy-done.4
  61.1 0.0 copy-done.7
  61.1 0.3 fusion.2
  61.5 7.9 %reduce-scatter.2.cloned.1.call-done = f32[16,32,128]{2,1,0:T(8,128)} async-done(((f32[32,32,128]{2,1,0:T(8,128)}), f32[16,32,128]{2,1,0:T(8,128)}) %reduce-scatter.2.cloned.1.call-update) | async-done | bytes 262160 | tf_op jit(solution)/shard_map/reduce_scatter | solution.py:40
  69.4 1.1 %bitcast_reduce_fusion = f32[32,16]{0,1:T(8,128)S(1)} fusion(f32[16,32,128]{2,1,0:T(8,128)} %reduce-scatter.2.cloned.1.call-done), kind=kLoop, calls=%fused_computation.30 | loop fusion | flops 65024 | bytes 264192 | tf_op jit(solution)/shard_map/reduce_sum | solution.py:8
  70.5 1.2 %multiply_reduce_fusion = f32[32,16]{0,1:T(8,128)S(1)} fusion(f32[16,32,128]{2,1,0:T(8,128)} %reduce-scatter.2.cloned.1.call-done, f32[32,16]{0,1:T(8,128)S(1)} %broadcast_multiply_fusion), kind=kLoop, calls=%fused_computation.32 | loop fusion | flops 196096 | bytes 266240 | tf_op jit(solution)/shard_map/reduce_sum | solution.py:10
  71.7 0.0 copy-done.5
  71.7 0.0 copy-done.6
  71.7 1.2 %add_convert_fusion = bf16[32,16,128]{2,0,1:T(8,128)(2,1)S(1)} fusion(f32[16,32,128]{2,1,0:T(8,128)} %reduce-scatter.2.cloned.1.call-done, f32[128]{0:T(128)S(1)} %copy-done.5, f32[128]{0:T(128)S(1)} %copy-done.6, f32[32,16]{0,1:T(8,128)S(1)} %add_rsqrt_fusion, f32[32,16]{0,1:T(8,128)S(1)} %broadcast_multiply_fusion), kind=kLoop, calls=%fused_computation.31 | loop fusion | flops 327680 | bytes 398336 | tf_op jit(solution)/shard_map/convert_element_type | solution.py:47
  72.9 0.0 copy-done.2
  72.9 0.8 %fusion.3 = bf16[32,16,128]{2,1,0:T(8,128)(2,1)} fusion(f32[32,16,128]{2,1,0:T(8,128)S(1)} %fusion.2, bf16[32,16,128]{2,0,1:T(8,128)(2,1)S(1)} %add_convert_fusion, bf16[128,128]{1,0:T(8,128)(2,1)S(1)} %copy-done.2), kind=kOutput, calls=%fused_computation.6 | convolution fusion | flops 16908288 | bytes 557056 | tf_op jit(solution)/shard_map/rwh,hc->rwc/dot_general | solution.py:51
  (4 shorter events, 0.0 us)
Async XLA Ops:
  6.5 3.3 %copy-start = (bf16[128,512]{1,0:T(8,128)(2,1)S(1)}, bf16[128,512]{1,0:T(8,128)(2,1)}, u32[]{:S(2)}) copy-start(bf16[128,512]{1,0:T(8,128)(2,1)} %param.13) | copy-start | bytes 393220
  29.3 22.6 %all-to-all-start = ((bf16[128,16,128]{2,1,0:T(8,128)(2,1)}), bf16[128,16,128]{2,1,0:T(8,128)(2,1)S(1)}, u32[]{:S(2)}, u32[]{:S(2)}) async-start(bf16[128,16,128]{2,1,0:T(8,128)(2,1)} %all_gather.7), calls=%async_computation | async-start | bytes 1048576 | tf_op jit(solution)/shard_map/all_to_all | solution.py:39
  33.1 36.3 %reduce-scatter.2.cloned.1.call-start = ((), (), s32[]{:S(2)}) async-start(), calls=%async_computation.2 | async-start | bytes 786432 | tf_op jit(solution)/shard_map/reduce_scatter | solution.py:40
  57.3 3.8 %copy-start.1 = (bf16[32,16,128]{2,1,0:T(8,128)(2,1)S(1)}, bf16[32,16,128]{2,1,0:T(8,128)(2,1)}, u32[]{:S(2)}) copy-start(bf16[32,16,128]{2,1,0:T(8,128)(2,1)} %param.9) | copy-start | bytes 393220
  57.3 3.8 %copy-start.3 = (f32[128]{0:T(128)S(1)}, f32[128]{0:T(128)}, u32[]{:S(2)}) copy-start(f32[128]{0:T(128)} %param.12) | copy-start | bytes 1540
  57.3 3.8 %copy-start.4 = (f32[128]{0:T(128)S(1)}, f32[128]{0:T(128)}, u32[]{:S(2)}) copy-start(f32[128]{0:T(128)} %param.11) | copy-start | bytes 1540
  57.3 3.8 %copy-start.7 = (bf16[128,128]{1,0:T(8,128)(2,1)S(1)}, bf16[128,128]{1,0:T(8,128)(2,1)}, u32[]{:S(2)}) copy-start(bf16[128,128]{1,0:T(8,128)(2,1)} %param.14) | copy-start | bytes 98308
  57.3 14.4 %copy-start.5 = (f32[128]{0:T(128)S(1)}, f32[128]{0:T(128)}, u32[]{:S(2)}) copy-start(f32[128]{0:T(128)} %param.16) | copy-start | bytes 1540
  57.4 14.4 %copy-start.6 = (f32[128]{0:T(128)S(1)}, f32[128]{0:T(128)}, u32[]{:S(2)}) copy-start(f32[128]{0:T(128)} %param.15) | copy-start | bytes 1540
  61.1 11.8 %copy-start.2 = (bf16[128,128]{1,0:T(8,128)(2,1)S(1)}, bf16[128,128]{1,0:T(8,128)(2,1)}, u32[]{:S(2)}) copy-start(bf16[128,128]{1,0:T(8,128)(2,1)} %param.17) | copy-start | bytes 98308
Sparse Core Ops, SparseCore 0:
  61.2 8.1 reduce-scatter.1
where the time goes:
time: 81.1 us; the launch traced here: 80.6 us
  blocking collectives  33.6 us (41%)
  between operations  13.6 us (17%)
  local copies, waits for them, and re-layouts  10.6 us (13%)
  waiting for transfers between devices  7.94 us (10%)
  other arithmetic  6.58 us (8%)
  matrix products  4.53 us (6%)
  starting transfers between devices  3.72 us (5%)
    all_gather x1, blocking collectives, on_device(): every_row = lax.all_gather(own_right, 'gx', axis=0, tiled=True)  18 us
    all_gather x1, blocking collectives, on_device(): lax.all_gather(left_side, 'gy', axis=1, tiled=True)  15.6 us
    reduce_scatter x1, waiting for transfers between devices, on_device(): lax.psum_scatter(jnp.einsum('jkc,ikc->jic', row_panel, left_slab, preferr...  7.92 us
    all_to_all x1, starting transfers between devices, on_device(): lax.all_to_all(every_row, 'gy', split_axis=0, concat_axis=1, tiled=True)  3.72 us
    transpose x1, local copies, waits for them, and re-layouts, on_device(): jnp.einsum('jkc,ikc->jic', row_panel, left_slab, preferred_element_type=j...  3.7 us
    all_to_all x2, local copies, waits for them, and re-layouts, on_device(): lax.all_to_all(every_row, 'gy', split_axis=0, concat_axis=1, tiled=True)  3.31 us
    all_gather x1, local copies, waits for them, and re-layouts, on_device(): lax.all_gather(left_side, 'gy', axis=1, tiled=True)  3.21 us
    reduce_sum x2, other arithmetic, normalize(): variance = jnp.mean(centered * centered, axis=-1, keepdims=True)  2.36 us
  transfers between devices with their start and end apart: 2, of which 1 were waited for; matrix products, arithmetic and copies ran while one was open for 4% of the time, Pallas kernels for 0%

commit v1 on v0

--- a/solution.py
+++ b/solution.py
@@ -1,14 +1,23 @@
+import functools
+
 import jax
 import jax.numpy as jnp
 from jax import lax
+from jax.experimental import pallas as pl
+from jax.experimental.pallas import tpu as pltpu
 from jax.sharding import PartitionSpec as P
+
+MESH = pl.DeviceIdType.MESH
+LANES = 128
+EPSILON = 1e-05
+PIECES = 4
 
 
 def normalize(values, gain, bias):
     average = jnp.mean(values, axis=-1, keepdims=True)
     centered = values - average
     variance = jnp.mean(centered * centered, axis=-1, keepdims=True)
-    return centered * lax.rsqrt(variance + 1e-05) * gain + bias
+    return centered * lax.rsqrt(variance + EPSILON) * gain + bias
 
 
 def project(tile, mask_value, in_gain, in_bias, proj_weight):
@@ -26,7 +35,7 @@
     return (normed, left_side, right_side)
 
 
-def on_device(
+def with_collectives(
     pair, pair_mask, in_gain, in_bias, proj_weight, gate_weight, out_gain, out_bias, out_weight
 ):
     mask_value = pair_mask.astype(jnp.float32)[:, :, None]
@@ -52,7 +61,293 @@
     return (gating * mixed).astype(jnp.bfloat16)
 
 
+def swap_groups(tiles, width):
+    tiles = list(tiles)
+    group = lax.broadcasted_iota(jnp.int32, tiles[0].shape, 1) // width
+    bit = 1
+    while bit < len(tiles):
+        upper = (group // bit) % 2 == 1
+        for a in range(len(tiles)):
+            if (a // bit) % 2 == 0:
+                low, high = tiles[a], tiles[a + bit]
+                tiles[a] = jnp.where(upper, pltpu.roll(high, bit * width, 1), low)
+                tiles[a + bit] = jnp.where(upper, high, pltpu.roll(low, LANES - bit * width, 1))
+        bit *= 2
+    return tiles
+
+
+def kernel(
+    nx,
+    ny,
+    nz,
+    pair_ref,
+    mask_ref,
+    in_gain_ref,
+    in_bias_ref,
+    proj_ref,
+    gate_ref,
+    out_gain_ref,
+    out_bias_ref,
+    out_weight_ref,
+    out_ref,
+    right_out,
+    left_out,
+    tri_out,
+    right_in,
+    left_in,
+    tri_in,
+    right_all,
+    left_all,
+    spread,
+    normed_ref,
+    gating_ref,
+    right_sems,
+    left_sems,
+    tri_sems,
+    z_send,
+    z_recv,
+):
+    rows, width, channels = pair_ref.shape
+    hidden = proj_ref.shape[1] // 4
+    plane = ny * nz
+    block = hidden // plane
+    tiles = rows * width // LANES
+    per_tile = rows // tiles
+    part = block // PIECES
+    x, y, z = lax.axis_index("gx"), lax.axis_index("gy"), lax.axis_index("gz")
+    me = y * nz + z
+
+    def peer(t):
+        d = lax.rem(me + t, plane)
+        return d, (x, d // nz, lax.rem(d, nz))
+
+    barrier = pltpu.get_barrier_semaphore()
+    for t in range(1, plane):
+        pl.semaphore_signal(barrier, inc=1, device_id=peer(t)[1], device_id_type=MESH)
+
+    @pl.when(x > 0)
+    def _():
+        pl.semaphore_signal(barrier, inc=1, device_id=(x - 1, y, z), device_id_type=MESH)
+
+    @pl.when(x < nx - 1)
+    def _():
+        pl.semaphore_signal(barrier, inc=1, device_id=(x + 1, y, z), device_id_type=MESH)
+
+    normed = normalize(
+        pair_ref[...].reshape(rows * width, channels).astype(jnp.float32),
+        in_gain_ref[...],
+        in_bias_ref[...],
+    ).astype(jnp.bfloat16)
+    normed_ref[...] = normed
+
+    spot = lax.broadcasted_iota(jnp.int32, (width, rows * width), 1)
+    choose = (spot % width == lax.broadcasted_iota(jnp.int32, spot.shape, 0)).astype(jnp.bfloat16)
+    repeated = jnp.dot(
+        mask_ref[...].astype(jnp.float32).astype(jnp.bfloat16), choose, preferred_element_type=jnp.float32
+    )
+    row_of = lax.broadcasted_iota(jnp.int32, repeated.shape, 1) // width
+    own_row = row_of == lax.broadcasted_iota(jnp.int32, repeated.shape, 0)
+    mask_row = jnp.sum(jnp.where(own_row, repeated, 0.0), axis=0, keepdims=True)
+
+    def side(first, target):
+        weight = proj_ref[:, first : first + 2 * hidden].T
+        for q in range(tiles):
+            lanes = slice(q * LANES, (q + 1) * LANES)
+            projected = lax.dot_general(
+                weight, normed_ref[lanes, :], (((1,), (1,)), ((), ())), preferred_element_type=jnp.float32
+            )
+            value = jax.nn.sigmoid(projected[:hidden]) * projected[hidden:] * mask_row[:, lanes]
+            target[:, q] = value.astype(jnp.bfloat16).reshape(plane, block, LANES)
+
+    def exchange(source, target, sems):
+        copies = []
+        for t in range(1, plane):
+            d, device = peer(t)
+            copies.append(
+                pltpu.make_async_remote_copy(
+                    src_ref=source.at[d],
+                    dst_ref=target.at[me],
+                    send_sem=sems.at[0, t],
+                    recv_sem=sems.at[1, t],
+                    device_id=device,
+                    device_id_type=MESH,
+                )
+            )
+            copies[-1].start()
+        return copies
+
+    def gather_sums(source, target):
+        for q in range(tiles):
+            swapped = swap_groups([source[a, q].astype(jnp.float32) for a in range(plane)], width)
+            for a in range(per_tile):
+                spread[pl.ds(q * per_tile + a, block, stride=rows), :] = swapped[a]
+        target[...] = spread[...].astype(jnp.bfloat16).reshape(block, rows, LANES)
+
+    side(2 * hidden, right_out)
+    pl.semaphore_wait(
+        barrier, plane - 1 + jnp.where(x > 0, 1, 0) + jnp.where(x < nx - 1, 1, 0)
+    )
+    right_copies = exchange(right_out, right_in, right_sems)
+    right_in[me] = right_out[me]
+    side(0, left_out)
+    left_copies = exchange(left_out, left_in, left_sems)
+    left_in[me] = left_out[me]
+    gating_ref[...] = jax.nn.sigmoid(
+        jnp.dot(normed_ref[...], gate_ref[...], preferred_element_type=jnp.float32)
+    )
+
+    for copy in right_copies:
+        copy.wait_recv()
+    gather_sums(right_in, right_all.at[x])
+
+    def pass_on(way, t, piece):
+        ahead = x + 1 if way == 0 else x - 1
+        origin = x - t if way == 0 else x + t
+        part_of = right_all.at[origin, pl.ds(piece * part, part)]
+        return pltpu.make_async_remote_copy(
+            src_ref=part_of,
+            dst_ref=part_of,
+            send_sem=z_send.at[way, t, piece],
+            recv_sem=z_recv.at[way, t, piece],
+            device_id=(ahead, y, z),
+            device_id_type=MESH,
+        )
+
+    def has_ahead(way):
+        return x < nx - 1 if way == 0 else x > 0
+
+    def has_origin(way, t):
+        return x >= t if way == 0 else x <= nx - 1 - t
+
+    for piece in range(PIECES):
+        for way in range(2):
+
+            @pl.when(has_ahead(way))
+            def _():
+                pass_on(way, 0, piece).start()
+
+    for copy in left_copies:
+        copy.wait_recv()
+    gather_sums(left_in, left_all)
+
+    for t in range(1, nx):
+        for piece in range(PIECES):
+            for way in range(2):
+
+                @pl.when(has_origin(way, t))
+                def _():
+                    pltpu.make_async_remote_copy(
+                        src_ref=right_all.at[x, pl.ds(piece * part, part)],
+                        dst_ref=right_all.at[x - t if way == 0 else x + t, pl.ds(piece * part, part)],
+                        send_sem=z_send.at[way, t - 1, piece],
+                        recv_sem=z_recv.at[way, t - 1, piece],
+                        device_id=(x, y, z),
+                        device_id_type=MESH,
+                    ).wait_recv()
+                    if t < nx - 1:
+
+                        @pl.when(has_ahead(way))
+                        def _():
+                            pass_on(way, t, piece).start()
+
+    for c in range(block):
+        triangle = lax.dot_general(
+            left_all[c],
+            right_all[:, c].reshape(nx * rows, LANES),
+            (((1,), (1,)), ((), ())),
+            preferred_element_type=jnp.float32,
+        )
+        spread[pl.ds(c, rows, stride=block), :] = triangle
+    for q in range(tiles):
+        swapped = swap_groups(
+            [spread[pl.ds((q * per_tile + a) * block, block), :] for a in range(per_tile)], width
+        )
+        for d in range(plane):
+            tri_out[d, q] = swapped[d].astype(jnp.bfloat16)
+    tri_copies = exchange(tri_out, tri_in, tri_sems)
+    tri_in[me] = tri_out[me]
+    for copy in tri_copies:
+        copy.wait_recv()
+
+    for q in range(tiles):
+        lanes = slice(q * LANES, (q + 1) * LANES)
+        sums = tri_in[:, q].reshape(hidden, LANES).astype(jnp.float32)
+        centered = sums - jnp.mean(sums, axis=0, keepdims=True)
+        variance = jnp.mean(centered * centered, axis=0, keepdims=True)
+        scaled = (centered * lax.rsqrt(variance + EPSILON)).T
+        tri_normed = (scaled * out_gain_ref[...] + out_bias_ref[...]).astype(jnp.bfloat16)
+        mixed = jnp.dot(tri_normed, out_weight_ref[...], preferred_element_type=jnp.float32)
+        out_ref[q * per_tile : (q + 1) * per_tile] = (
+            (gating_ref[lanes, :] * mixed).astype(jnp.bfloat16).reshape(per_tile, width, channels)
+        )
+
+    for copies in (right_copies, left_copies, tri_copies):
+        for copy in copies:
+            copy.wait_send()
+    for t in range(nx - 1):
+        for piece in range(PIECES):
+            for way in range(2):
+
+                @pl.when(jnp.logical_and(has_ahead(way), has_origin(way, t)))
+                def _():
+                    pass_on(way, t, piece).wait_send()
+
+
+def fused(nx, ny, nz, *arguments):
+    pair, pair_mask, in_gain, in_bias, proj_weight, gate_weight, out_gain, out_bias, out_weight = arguments
+    rows, width, channels = pair.shape
+    hidden = proj_weight.shape[1] // 4
+    plane = ny * nz
+    block = hidden // plane
+    tiles = rows * width // LANES
+    travelling = pltpu.VMEM((plane, tiles, block, LANES), jnp.bfloat16)
+    return pl.pallas_call(
+        functools.partial(kernel, nx, ny, nz),
+        out_shape=jax.ShapeDtypeStruct(pair.shape, jnp.bfloat16),
+        in_specs=[pl.BlockSpec(memory_space=pltpu.VMEM)] * 9,
+        out_specs=pl.BlockSpec(memory_space=pltpu.VMEM),
+        scratch_shapes=[travelling] * 6
+        + [
+            pltpu.VMEM((nx, block, rows, LANES), jnp.bfloat16),
+            pltpu.VMEM((block, rows, LANES), jnp.bfloat16),
+            pltpu.VMEM((block * rows, LANES), jnp.float32),
+            pltpu.VMEM((rows * width, channels), jnp.bfloat16),
+            pltpu.VMEM((rows * width, channels), jnp.float32),
+        ]
+        + [pltpu.SemaphoreType.DMA((2, plane))] * 3
+        + [pltpu.SemaphoreType.DMA((2, nx - 1, PIECES))] * 2,
+        compiler_params=pltpu.CompilerParams(collective_id=0, has_side_effects=True),
+    )(
+        pair,
+        pair_mask,
+        in_gain.reshape(1, -1),
+        in_bias.reshape(1, -1),
+        proj_weight,
+        gate_weight,
+        out_gain.reshape(1, -1),
+        out_bias.reshape(1, -1),
+        out_weight,
+    )
+
+
 def solution(mesh):
+    nx, ny, nz = mesh.shape["gx"], mesh.shape["gy"], mesh.shape["gz"]
+    plane = ny * nz
+
+    def on_device(pair, *others):
+        rows, width, channels = pair.shape
+        hidden = others[3].shape[1] // 4
+        fits = (
+            width * plane == LANES
+            and rows * nx == LANES
+            and rows % plane == 0
+            and channels % LANES == 0
+            and hidden % (16 * plane) == 0
+        )
+        if fits:
+            return fused(nx, ny, nz, pair, *others)
+        return with_collectives(pair, *others)
+
     return jax.shard_map(
         on_device,
         mesh=mesh,

time: 81.1 us -> 30.9 us (0.38)
  blocking collectives: 33.6 us -> 0 us
  Pallas kernels: 0 us -> 27.8 us
  between operations: 13.6 us -> 0.01 us
  waiting for transfers between devices: 7.94 us -> 0 us
  local copies, waits for them, and re-layouts: 10.6 us -> 2.94 us
  other arithmetic: 6.58 us -> 0 us
  matrix products: 4.53 us -> 0 us
  starting transfers between devices: 3.72 us -> 0 us
    all_gather x2 -> x0, blocking collectives: 33.6 us -> none  [the longest x1 18 us: on_device(): every_row = lax.all_gather(own_right, 'gx', axis=0, tiled=True)]
    pallas_call x0 -> x1, Pallas kernels: none -> 27.8 us  [fused(): pl.pallas_call(functools.partial(kernel, nx, ny, nz), out_shape=jax.Shape...]
    reduce_scatter x1 -> x0, waiting for transfers between devices: 7.92 us -> none  [on_device(): lax.psum_scatter(jnp.einsum('jkc,ikc->jic', row_panel, left_slab, preferr...]
    dot_general x4 -> x0, matrix products: 4.53 us -> none  [the longest x1 2.08 us: on_device(): jnp.einsum('jkc,ikc->jic', row_panel, left_slab, preferred_element_type=j...]
    reduce_sum x4 -> x0, other arithmetic: 4.52 us -> none  [the longest x2 2.36 us: normalize(): variance = jnp.mean(centered * centered, axis=-1, keepdims=True)]
    all_to_all x1 -> x0, starting transfers between devices: 3.72 us -> none  [on_device(): lax.all_to_all(every_row, 'gy', split_axis=0, concat_axis=1, tiled=True)]
    transpose x1 -> x0, local copies, waits for them, and re-layouts: 3.7 us -> none  [on_device(): jnp.einsum('jkc,ikc->jic', row_panel, left_slab, preferred_element_type=j...]
    all_to_all x2 -> x0, local copies, waits for them, and re-layouts: 3.31 us -> none  [on_device(): lax.all_to_all(every_row, 'gy', split_axis=0, concat_axis=1, tiled=True)]
  transfers between devices with their start and end apart: 2 -> 0, of which waited for: 1 -> 0; matrix products, arithmetic and copies ran while one was open for 4% -> 0% of each run, Pallas kernels for 0% -> 0%
where the time goes in v1:
time: 30.9 us; the launch traced here: 30.7 us
  Pallas kernels  27.8 us (90%)
  local copies, waits for them, and re-layouts  2.94 us (10%)
    pallas_call x1, Pallas kernels, fused(): pl.pallas_call(functools.partial(kernel, nx, ny, nz), out_shape=jax.Shape...  27.8 us
    unnamed x2, local copies, waits for them, and re-layouts  2.94 us

profile of v1, /device:TPU:0, one launch (start us, length us, event | category | flops | bytes accessed | tf_op | source)
XLA Modules:
  0.0 30.7 jit_solution(6178392160301821841)
XLA Ops:
  0.0 1.4 %copy.10.mask_ref = s32[32,16]{1,0:T(8,128)} copy(s32[32,16]{0,1:T(8,128)} %param.10) | data formatting | bytes 4096 | tf_op args[1]
  1.4 27.8 %shard_map.91 = bf16[32,16,128]{2,1,0:T(8,128)(2,1)} custom-call(bf16[32,16,128]{2,1,0:T(8,128)(2,1)} %pair_ref.1, s32[32,16]{1,0:T(8,128)} %copy.10.mask_ref, f32[1,128]{1,0:T(1,128)} %bitcast.4, f32[1,128]{1,0:T(1,128)} %bitcast.5, bf16[128,512]{1,0:T(8,128)(2,1)} %proj_ref.1, bf16[128,128]{1,0:T(8,128)(2,1)} %gate_ref.1, f32[1,128]{1,0:T(1,128)} %bitcast.6, ...), custom_call_target="tpu_custom_call" | custom-call | tf_op jit(solution)/shard_map/pallas_call | solution.py:304
  29.1 1.6 %copy.12 = bf16[32,16,128]{2,1,0:T(8,128)(2,1)} copy(bf16[32,16,128]{2,1,0:T(8,128)(2,1)} %shard_map.91) | data formatting | bytes 262144

commit v2 on v1

--- a/solution.py
+++ b/solution.py
@@ -98,6 +98,8 @@
     tri_in,
     right_all,
     left_all,
+    left_far,
+    tri_far,
     spread,
     normed_ref,
     gating_ref,
@@ -106,6 +108,8 @@
     tri_sems,
     z_send,
     z_recv,
+    far_sems,
+    far_send,
 ):
     rows, width, channels = pair_ref.shape
     hidden = proj_ref.shape[1] // 4
@@ -116,6 +120,15 @@
     part = block // PIECES
     x, y, z = lax.axis_index("gx"), lax.axis_index("gy"), lax.axis_index("gz")
     me = y * nz + z
+    owners = rows // width
+    is_end = jnp.logical_or(x == 0, x == nx - 1)
+    is_helper = jnp.logical_or(x == 1, x == nx - 2)
+    end = jnp.where(x < nx // 2, 0, nx - 1)
+    helper = jnp.where(x < nx // 2, 1, nx - 2)
+
+    def is_left_out(d):
+        return jnp.logical_and(is_end, d // owners == nx - 1 - end)
+
 
     def peer(t):
         d = lax.rem(me + t, plane)
@@ -132,6 +145,13 @@
     @pl.when(x < nx - 1)
     def _():
         pl.semaphore_signal(barrier, inc=1, device_id=(x + 1, y, z), device_id_type=MESH)
+
+    @pl.when(is_left_out(me))
+    def _():
+        for t in range(plane):
+            d = lax.rem(me + t, plane)
+            device = (helper, d // nz, lax.rem(d, nz))
+            pl.semaphore_signal(barrier, inc=1, device_id=device, device_id_type=MESH)
 
     normed = normalize(
         pair_ref[...].reshape(rows * width, channels).astype(jnp.float32),
@@ -140,14 +160,14 @@
     ).astype(jnp.bfloat16)
     normed_ref[...] = normed
 
-    spot = lax.broadcasted_iota(jnp.int32, (width, rows * width), 1)
-    choose = (spot % width == lax.broadcasted_iota(jnp.int32, spot.shape, 0)).astype(jnp.bfloat16)
+    row_of = lax.broadcasted_iota(jnp.int32, (rows, rows * width), 1) // width
+    choose = (row_of == lax.broadcasted_iota(jnp.int32, row_of.shape, 0)).astype(jnp.bfloat16)
     repeated = jnp.dot(
         mask_ref[...].astype(jnp.float32).astype(jnp.bfloat16), choose, preferred_element_type=jnp.float32
     )
-    row_of = lax.broadcasted_iota(jnp.int32, repeated.shape, 1) // width
-    own_row = row_of == lax.broadcasted_iota(jnp.int32, repeated.shape, 0)
-    mask_row = jnp.sum(jnp.where(own_row, repeated, 0.0), axis=0, keepdims=True)
+    column_of = lax.broadcasted_iota(jnp.int32, repeated.shape, 1) % width
+    own_column = column_of == lax.broadcasted_iota(jnp.int32, repeated.shape, 0)
+    mask_row = jnp.sum(jnp.where(own_column, repeated, 0.0), axis=0, keepdims=True)
 
     def side(first, target):
         weight = proj_ref[:, first : first + 2 * hidden].T
@@ -185,7 +205,7 @@
 
     side(2 * hidden, right_out)
     pl.semaphore_wait(
-        barrier, plane - 1 + jnp.where(x > 0, 1, 0) + jnp.where(x < nx - 1, 1, 0)
+        barrier, jnp.where(is_end, plane, jnp.where(is_helper, plane + 1 + owners, plane + 1))
     )
     right_copies = exchange(right_out, right_in, right_sems)
     right_in[me] = right_out[me]
@@ -230,7 +250,21 @@
         copy.wait_recv()
     gather_sums(left_in, left_all)
 
-    for t in range(1, nx):
+    left_copy = pltpu.make_async_remote_copy(
+        src_ref=left_all,
+        dst_ref=left_far,
+        send_sem=far_sems.at[0],
+        recv_sem=far_sems.at[1],
+        device_id=(helper, y, z),
+        device_id_type=MESH,
+    )
+
+    @pl.when(is_end)
+    def _():
+        left_copy.start()
+        right_all[nx - 1 - end] = jnp.zeros(right_all.shape[1:], right_all.dtype)
+
+    for t in range(1, nx - 1):
         for piece in range(PIECES):
             for way in range(2):
 
@@ -244,30 +278,74 @@
                         device_id=(x, y, z),
                         device_id_type=MESH,
                     ).wait_recv()
-                    if t < nx - 1:
+                    if t < nx - 2:
 
                         @pl.when(has_ahead(way))
                         def _():
                             pass_on(way, t, piece).start()
 
-    for c in range(block):
-        triangle = lax.dot_general(
-            left_all[c],
-            right_all[:, c].reshape(nx * rows, LANES),
-            (((1,), (1,)), ((), ())),
-            preferred_element_type=jnp.float32,
+    def multiply(left, target):
+        for c in range(block):
+            triangle = lax.dot_general(
+                left[c],
+                right_all[:, c].reshape(nx * rows, LANES),
+                (((1,), (1,)), ((), ())),
+                preferred_element_type=jnp.float32,
+            )
+            spread[pl.ds(c, rows, stride=block), :] = triangle
+        for q in range(tiles):
+            swapped = swap_groups(
+                [spread[pl.ds((q * per_tile + a) * block, block), :] for a in range(per_tile)], width
+            )
+            for d in range(plane):
+                target[d, q] = swapped[d].astype(jnp.bfloat16)
+
+    def far_copy(index):
+        d = (nx - 1 - end) * owners + index
+        return pltpu.make_async_remote_copy(
+            src_ref=tri_far.at[d],
+            dst_ref=tri_in.at[me],
+            send_sem=far_send.at[index],
+            recv_sem=tri_sems.at[1, lax.rem(d - me + plane, plane)],
+            device_id=(end, d // nz, lax.rem(d, nz)),
+            device_id_type=MESH,
         )
-        spread[pl.ds(c, rows, stride=block), :] = triangle
-    for q in range(tiles):
-        swapped = swap_groups(
-            [spread[pl.ds((q * per_tile + a) * block, block), :] for a in range(per_tile)], width
+
+    def tri_copy(t):
+        d, device = peer(t)
+        return pltpu.make_async_remote_copy(
+            src_ref=tri_out.at[d],
+            dst_ref=tri_in.at[me],
+            send_sem=tri_sems.at[0, t],
+            recv_sem=tri_sems.at[1, t],
+            device_id=device,
+            device_id_type=MESH,
         )
-        for d in range(plane):
-            tri_out[d, q] = swapped[d].astype(jnp.bfloat16)
-    tri_copies = exchange(tri_out, tri_in, tri_sems)
-    tri_in[me] = tri_out[me]
-    for copy in tri_copies:
-        copy.wait_recv()
+
+    @pl.when(is_helper)
+    def _():
+        left_copy.wait_recv()
+        multiply(left_far, tri_far)
+        for index in range(owners):
+            far_copy(index).start()
+
+    multiply(left_all, tri_out)
+    for t in range(1, plane):
+
+        @pl.when(jnp.logical_not(is_left_out(peer(t)[0])))
+        def _():
+            tri_copy(t).start()
+
+    @pl.when(jnp.logical_not(is_left_out(me)))
+    def _():
+        tri_in[me] = tri_out[me]
+
+    @pl.when(is_left_out(me))
+    def _():
+        tri_copy(0).wait_recv()
+
+    for t in range(1, plane):
+        tri_copy(t).wait_recv()
 
     for q in range(tiles):
         lanes = slice(q * LANES, (q + 1) * LANES)
@@ -281,10 +359,24 @@
             (gating_ref[lanes, :] * mixed).astype(jnp.bfloat16).reshape(per_tile, width, channels)
         )
 
-    for copies in (right_copies, left_copies, tri_copies):
-        for copy in copies:
-            copy.wait_send()
-    for t in range(nx - 1):
+    for copy in right_copies + left_copies:
+        copy.wait_send()
+    for t in range(1, plane):
+
+        @pl.when(jnp.logical_not(is_left_out(peer(t)[0])))
+        def _():
+            tri_copy(t).wait_send()
+
+    @pl.when(is_helper)
+    def _():
+        for index in range(owners):
+            far_copy(index).wait_send()
+
+    @pl.when(is_end)
+    def _():
+        left_copy.wait_send()
+
+    for t in range(nx - 2):
         for piece in range(PIECES):
             for way in range(2):
 
@@ -310,16 +402,19 @@
         + [
             pltpu.VMEM((nx, block, rows, LANES), jnp.bfloat16),
             pltpu.VMEM((block, rows, LANES), jnp.bfloat16),
+            pltpu.VMEM((block, rows, LANES), jnp.bfloat16),
+            travelling,
             pltpu.VMEM((block * rows, LANES), jnp.float32),
             pltpu.VMEM((rows * width, channels), jnp.bfloat16),
             pltpu.VMEM((rows * width, channels), jnp.float32),
         ]
         + [pltpu.SemaphoreType.DMA((2, plane))] * 3
-        + [pltpu.SemaphoreType.DMA((2, nx - 1, PIECES))] * 2,
+        + [pltpu.SemaphoreType.DMA((2, nx - 2, PIECES))] * 2
+        + [pltpu.SemaphoreType.DMA((2,)), pltpu.SemaphoreType.DMA((rows // width,))],
         compiler_params=pltpu.CompilerParams(collective_id=0, has_side_effects=True),
     )(
         pair,
-        pair_mask,
+        pair_mask.T,
         in_gain.reshape(1, -1),
         in_bias.reshape(1, -1),
         proj_weight,
@@ -341,6 +436,8 @@
             width * plane == LANES
             and rows * nx == LANES
             and rows % plane == 0
+            and rows % width == 0
+            and nx >= 4
             and channels % LANES == 0
             and hidden % (16 * plane) == 0
         )

time: 30.9 us -> 25.9 us (0.84)
  Pallas kernels: 27.8 us -> 24.1 us
  local copies, waits for them, and re-layouts: 2.94 us -> 1.57 us
    pallas_call x1, Pallas kernels: 27.8 us -> 24.1 us  [fused(): pl.pallas_call(functools.partial(kernel, nx, ny, nz), out_shape=jax.Shape...]
    unnamed x2 -> x1, local copies, waits for them, and re-layouts: 2.94 us -> 1.57 us
where the time goes in v2:
time: 25.9 us; the launch traced here: 25.7 us
  Pallas kernels  24.1 us (93%)
  local copies, waits for them, and re-layouts  1.57 us (6%)
    pallas_call x1, Pallas kernels, fused(): pl.pallas_call(functools.partial(kernel, nx, ny, nz), out_shape=jax.Shape...  24.1 us
    unnamed x1, local copies, waits for them, and re-layouts  1.57 us

profile of v2, /device:TPU:0, one launch (start us, length us, event | category | flops | bytes accessed | tf_op | source)
XLA Modules:
  0.0 25.7 jit_solution(3660157047604098524)
XLA Ops:
  0.0 24.1 %shard_map.91 = bf16[32,16,128]{2,1,0:T(8,128)(2,1)} custom-call(bf16[32,16,128]{2,1,0:T(8,128)(2,1)} %pair_ref.1, s32[16,32]{1,0:T(8,128)} %bitcast.5, f32[1,128]{1,0:T(1,128)} %bitcast.6, f32[1,128]{1,0:T(1,128)} %bitcast.7, bf16[128,512]{1,0:T(8,128)(2,1)} %proj_ref.1, bf16[128,128]{1,0:T(8,128)(2,1)} %gate_ref.1, f32[1,128]{1,0:T(1,128)} %bitcast.8, ...), custom_call_target="tpu_custom_call" | custom-call | tf_op jit(solution)/shard_map/pallas_call | solution.py:396
  24.1 1.6 %copy.11 = bf16[32,16,128]{2,1,0:T(8,128)(2,1)} copy(bf16[32,16,128]{2,1,0:T(8,128)(2,1)} %shard_map.91) | data formatting | bytes 262144

commit v3 on v2

--- a/solution.py
+++ b/solution.py
@@ -80,15 +80,15 @@
     nx,
     ny,
     nz,
-    pair_ref,
-    mask_ref,
-    in_gain_ref,
-    in_bias_ref,
-    proj_ref,
-    gate_ref,
-    out_gain_ref,
-    out_bias_ref,
-    out_weight_ref,
+    pair_hbm,
+    mask_hbm,
+    in_gain_hbm,
+    in_bias_hbm,
+    proj_hbm,
+    gate_hbm,
+    out_gain_hbm,
+    out_bias_hbm,
+    out_weight_hbm,
     out_ref,
     right_out,
     left_out,
@@ -110,6 +110,16 @@
     z_recv,
     far_sems,
     far_send,
+    pair_ref,
+    mask_ref,
+    in_gain_ref,
+    in_bias_ref,
+    proj_ref,
+    gate_ref,
+    out_gain_ref,
+    out_bias_ref,
+    out_weight_ref,
+    load_sems,
 ):
     rows, width, channels = pair_ref.shape
     hidden = proj_ref.shape[1] // 4
@@ -134,6 +144,23 @@
         d = lax.rem(me + t, plane)
         return d, (x, d // nz, lax.rem(d, nz))
 
+    arguments = (
+        (pair_hbm, pair_ref),
+        (mask_hbm, mask_ref),
+        (in_gain_hbm, in_gain_ref),
+        (in_bias_hbm, in_bias_ref),
+        (proj_hbm, proj_ref),
+        (gate_hbm, gate_ref),
+        (out_gain_hbm, out_gain_ref),
+        (out_bias_hbm, out_bias_ref),
+        (out_weight_hbm, out_weight_ref),
+    )
+    loads = [
+        pltpu.make_async_copy(held, wanted, load_sems.at[index])
+        for index, (held, wanted) in enumerate(arguments)
+    ]
+    for load in loads:
+        load.start()
     barrier = pltpu.get_barrier_semaphore()
     for t in range(1, plane):
         pl.semaphore_signal(barrier, inc=1, device_id=peer(t)[1], device_id_type=MESH)
@@ -153,6 +180,8 @@
             device = (helper, d // nz, lax.rem(d, nz))
             pl.semaphore_signal(barrier, inc=1, device_id=device, device_id_type=MESH)
 
+    for load in (loads[0], loads[2], loads[3]):
+        load.wait()
     normed = normalize(
         pair_ref[...].reshape(rows * width, channels).astype(jnp.float32),
         in_gain_ref[...],
@@ -160,6 +189,7 @@
     ).astype(jnp.bfloat16)
     normed_ref[...] = normed
 
+    loads[1].wait()
     row_of = lax.broadcasted_iota(jnp.int32, (rows, rows * width), 1) // width
     choose = (row_of == lax.broadcasted_iota(jnp.int32, row_of.shape, 0)).astype(jnp.bfloat16)
     repeated = jnp.dot(
@@ -203,6 +233,7 @@
                 spread[pl.ds(q * per_tile + a, block, stride=rows), :] = swapped[a]
         target[...] = spread[...].astype(jnp.bfloat16).reshape(block, rows, LANES)
 
+    loads[4].wait()
     side(2 * hidden, right_out)
     pl.semaphore_wait(
         barrier, jnp.where(is_end, plane, jnp.where(is_helper, plane + 1 + owners, plane + 1))
@@ -212,6 +243,7 @@
     side(0, left_out)
     left_copies = exchange(left_out, left_in, left_sems)
     left_in[me] = left_out[me]
+    loads[5].wait()
     gating_ref[...] = jax.nn.sigmoid(
         jnp.dot(normed_ref[...], gate_ref[...], preferred_element_type=jnp.float32)
     )
@@ -347,6 +379,8 @@
     for t in range(1, plane):
         tri_copy(t).wait_recv()
 
+    for load in loads[6:]:
+        load.wait()
     for q in range(tiles):
         lanes = slice(q * LANES, (q + 1) * LANES)
         sums = tri_in[:, q].reshape(hidden, LANES).astype(jnp.float32)
@@ -396,7 +430,7 @@
     return pl.pallas_call(
         functools.partial(kernel, nx, ny, nz),
         out_shape=jax.ShapeDtypeStruct(pair.shape, jnp.bfloat16),
-        in_specs=[pl.BlockSpec(memory_space=pltpu.VMEM)] * 9,
+        in_specs=[pl.BlockSpec(memory_space=pltpu.HBM)] * 9,
         out_specs=pl.BlockSpec(memory_space=pltpu.VMEM),
         scratch_shapes=[travelling] * 6
         + [
@@ -410,7 +444,19 @@
         ]
         + [pltpu.SemaphoreType.DMA((2, plane))] * 3
         + [pltpu.SemaphoreType.DMA((2, nx - 2, PIECES))] * 2
-        + [pltpu.SemaphoreType.DMA((2,)), pltpu.SemaphoreType.DMA((rows // width,))],
+        + [pltpu.SemaphoreType.DMA((2,)), pltpu.SemaphoreType.DMA((rows // width,))]
+        + [
+            pltpu.VMEM(pair.shape, pair.dtype),
+            pltpu.VMEM((width, rows), pair_mask.dtype),
+            pltpu.VMEM((1, in_gain.size), in_gain.dtype),
+            pltpu.VMEM((1, in_bias.size), in_bias.dtype),
+            pltpu.VMEM(proj_weight.shape, proj_weight.dtype),
+            pltpu.VMEM(gate_weight.shape, gate_weight.dtype),
+            pltpu.VMEM((1, out_gain.size), out_gain.dtype),
+            pltpu.VMEM((1, out_bias.size), out_bias.dtype),
+            pltpu.VMEM(out_weight.shape, out_weight.dtype),
+            pltpu.SemaphoreType.DMA((9,)),
+        ],
         compiler_params=pltpu.CompilerParams(collective_id=0, has_side_effects=True),
     )(
         pair,

time: 25.9 us -> 24.9 us (0.961)
  Pallas kernels: 24.1 us -> 23.2 us
    pallas_call x1, Pallas kernels: 24.1 us -> 23.2 us  [fused(): pl.pallas_call(functools.partial(kernel, nx, ny, nz), out_shape=jax.Shape...]
where the time goes in v3:
time: 24.9 us; the launch traced here: 24.8 us
  Pallas kernels  23.2 us (93%)
  local copies, waits for them, and re-layouts  1.57 us (6%)
    pallas_call x1, Pallas kernels, fused(): pl.pallas_call(functools.partial(kernel, nx, ny, nz), out_shape=jax.Shape...  23.2 us
    unnamed x1, local copies, waits for them, and re-layouts  1.57 us

profile of v3, /device:TPU:0, one launch (start us, length us, event | category | flops | bytes accessed | tf_op | source)
XLA Modules:
  0.0 24.8 jit_solution(1689853710179083521)
XLA Ops:
  0.0 23.2 %shard_map.91 = bf16[32,16,128]{2,1,0:T(8,128)(2,1)} custom-call(bf16[32,16,128]{2,1,0:T(8,128)(2,1)} %pair_hbm.1, s32[16,32]{1,0:T(8,128)} %bitcast.5, f32[1,128]{1,0:T(1,128)} %bitcast.6, f32[1,128]{1,0:T(1,128)} %bitcast.7, bf16[128,512]{1,0:T(8,128)(2,1)} %proj_hbm.1, bf16[128,128]{1,0:T(8,128)(2,1)} %gate_hbm.1, f32[1,128]{1,0:T(1,128)} %bitcast.8, ...), custom_call_target="tpu_custom_call" | custom-call | tf_op jit(solution)/shard_map/pallas_call | solution.py:430
  23.2 1.6 %copy.11 = bf16[32,16,128]{2,1,0:T(8,128)(2,1)} copy(bf16[32,16,128]{2,1,0:T(8,128)(2,1)} %shard_map.91) | data formatting | bytes 262144

commit v4 on v3

--- a/solution.py
+++ b/solution.py
@@ -10,7 +10,9 @@
 MESH = pl.DeviceIdType.MESH
 LANES = 128
 EPSILON = 1e-05
-PIECES = 4
+PARTS = 2
+RIGHT_STEPS = 2
+TRI_STEPS = 1
 
 
 def normalize(values, gain, bias):
@@ -127,7 +129,8 @@
     block = hidden // plane
     tiles = rows * width // LANES
     per_tile = rows // tiles
-    part = block // PIECES
+    per_step = tiles // TRI_STEPS
+    part = block // PARTS
     x, y, z = lax.axis_index("gx"), lax.axis_index("gy"), lax.axis_index("gz")
     me = y * nz + z
     owners = rows // width
@@ -182,12 +185,15 @@
 
     for load in (loads[0], loads[2], loads[3]):
         load.wait()
-    normed = normalize(
-        pair_ref[...].reshape(rows * width, channels).astype(jnp.float32),
-        in_gain_ref[...],
-        in_bias_ref[...],
-    ).astype(jnp.bfloat16)
-    normed_ref[...] = normed
+
+    def norm(step):
+        some = slice(step * rows // RIGHT_STEPS, (step + 1) * rows // RIGHT_STEPS)
+        pairs = slice(some.start * width, some.stop * width)
+        normed_ref[pairs, :] = normalize(
+            pair_ref[some].reshape(-1, channels).astype(jnp.float32), in_gain_ref[...], in_bias_ref[...]
+        ).astype(jnp.bfloat16)
+
+    norm(0)
 
     loads[1].wait()
     row_of = lax.broadcasted_iota(jnp.int32, (rows, rows * width), 1) // width
@@ -199,9 +205,8 @@
     own_column = column_of == lax.broadcasted_iota(jnp.int32, repeated.shape, 0)
     mask_row = jnp.sum(jnp.where(own_column, repeated, 0.0), axis=0, keepdims=True)
 
-    def side(first, target):
-        weight = proj_ref[:, first : first + 2 * hidden].T
-        for q in range(tiles):
+    def side(weight, target, step, steps):
+        for q in range(step * tiles // steps, (step + 1) * tiles // steps):
             lanes = slice(q * LANES, (q + 1) * LANES)
             projected = lax.dot_general(
                 weight, normed_ref[lanes, :], (((1,), (1,)), ((), ())), preferred_element_type=jnp.float32
@@ -209,53 +214,69 @@
             value = jax.nn.sigmoid(projected[:hidden]) * projected[hidden:] * mask_row[:, lanes]
             target[:, q] = value.astype(jnp.bfloat16).reshape(plane, block, LANES)
 
-    def exchange(source, target, sems):
+    def exchange(source, target, sems, step, steps):
+        count = tiles // steps
         copies = []
         for t in range(1, plane):
             d, device = peer(t)
             copies.append(
                 pltpu.make_async_remote_copy(
-                    src_ref=source.at[d],
-                    dst_ref=target.at[me],
-                    send_sem=sems.at[0, t],
-                    recv_sem=sems.at[1, t],
+                    src_ref=source.at[d, pl.ds(step * count, count)],
+                    dst_ref=target.at[me, pl.ds(step * count, count)],
+                    send_sem=sems.at[0, step, t],
+                    recv_sem=sems.at[1, step, t],
                     device_id=device,
                     device_id_type=MESH,
                 )
             )
             copies[-1].start()
+        target[me, step * count : (step + 1) * count] = source[me, step * count : (step + 1) * count]
         return copies
 
-    def gather_sums(source, target):
-        for q in range(tiles):
+    def gather_sums(source, target, step, steps):
+        some = rows // steps
+        for index, q in enumerate(range(step * tiles // steps, (step + 1) * tiles // steps)):
             swapped = swap_groups([source[a, q].astype(jnp.float32) for a in range(plane)], width)
             for a in range(per_tile):
-                spread[pl.ds(q * per_tile + a, block, stride=rows), :] = swapped[a]
-        target[...] = spread[...].astype(jnp.bfloat16).reshape(block, rows, LANES)
+                first = step * some * block + index * per_tile + a
+                spread[pl.ds(first, block, stride=some), :] = swapped[a]
+        target[:, step * some : (step + 1) * some] = (
+            spread[step * some * block : (step + 1) * some * block]
+            .astype(jnp.bfloat16)
+            .reshape(block, some, LANES)
+        )
 
     loads[4].wait()
-    side(2 * hidden, right_out)
-    pl.semaphore_wait(
-        barrier, jnp.where(is_end, plane, jnp.where(is_helper, plane + 1 + owners, plane + 1))
-    )
-    right_copies = exchange(right_out, right_in, right_sems)
-    right_in[me] = right_out[me]
-    side(0, left_out)
-    left_copies = exchange(left_out, left_in, left_sems)
-    left_in[me] = left_out[me]
+    right_weight = proj_ref[:, 2 * hidden :].T
+    right_copies = []
+    for step in range(RIGHT_STEPS):
+        if step > 0:
+            norm(step)
+        side(right_weight, right_out, step, RIGHT_STEPS)
+        if step == 0:
+            pl.semaphore_wait(
+                barrier, jnp.where(is_end, plane, jnp.where(is_helper, plane + 1 + owners, plane + 1))
+            )
+        right_copies.append(exchange(right_out, right_in, right_sems, step, RIGHT_STEPS))
+    side(proj_ref[:, : 2 * hidden].T, left_out, 0, 1)
+    left_copies = exchange(left_out, left_in, left_sems, 0, 1)
     loads[5].wait()
     gating_ref[...] = jax.nn.sigmoid(
         jnp.dot(normed_ref[...], gate_ref[...], preferred_element_type=jnp.float32)
     )
 
-    for copy in right_copies:
-        copy.wait_recv()
-    gather_sums(right_in, right_all.at[x])
+    pieces = RIGHT_STEPS * PARTS
+
+    def piece_of(origin, piece):
+        some = rows // RIGHT_STEPS
+        return right_all.at[
+            origin, pl.ds(piece % PARTS * part, part), pl.ds(piece // PARTS * some, some)
+        ]
 
     def pass_on(way, t, piece):
         ahead = x + 1 if way == 0 else x - 1
         origin = x - t if way == 0 else x + t
-        part_of = right_all.at[origin, pl.ds(piece * part, part)]
+        part_of = piece_of(origin, piece)
         return pltpu.make_async_remote_copy(
             src_ref=part_of,
             dst_ref=part_of,
@@ -271,16 +292,20 @@
     def has_origin(way, t):
         return x >= t if way == 0 else x <= nx - 1 - t
 
-    for piece in range(PIECES):
-        for way in range(2):
-
-            @pl.when(has_ahead(way))
-            def _():
-                pass_on(way, 0, piece).start()
+    for step in range(RIGHT_STEPS):
+        for copy in right_copies[step]:
+            copy.wait_recv()
+        gather_sums(right_in, right_all.at[x], step, RIGHT_STEPS)
+        for piece in range(step * PARTS, (step + 1) * PARTS):
+            for way in range(2):
+
+                @pl.when(has_ahead(way))
+                def _():
+                    pass_on(way, 0, piece).start()
 
     for copy in left_copies:
         copy.wait_recv()
-    gather_sums(left_in, left_all)
+    gather_sums(left_in, left_all, 0, 1)
 
     left_copy = pltpu.make_async_remote_copy(
         src_ref=left_all,
@@ -297,14 +322,14 @@
         right_all[nx - 1 - end] = jnp.zeros(right_all.shape[1:], right_all.dtype)
 
     for t in range(1, nx - 1):
-        for piece in range(PIECES):
+        for piece in range(pieces):
             for way in range(2):
 
                 @pl.when(has_origin(way, t))
                 def _():
                     pltpu.make_async_remote_copy(
-                        src_ref=right_all.at[x, pl.ds(piece * part, part)],
-                        dst_ref=right_all.at[x - t if way == 0 else x + t, pl.ds(piece * part, part)],
+                        src_ref=piece_of(x, piece),
+                        dst_ref=piece_of(x - t if way == 0 else x + t, piece),
                         send_sem=z_send.at[way, t - 1, piece],
                         recv_sem=z_recv.at[way, t - 1, piece],
                         device_id=(x, y, z),
@@ -316,7 +341,7 @@
                         def _():
                             pass_on(way, t, piece).start()
 
-    def multiply(left, target):
+    def multiply(left, target, send):
         for c in range(block):
             triangle = lax.dot_general(
                 left[c],
@@ -331,57 +356,66 @@
             )
             for d in range(plane):
                 target[d, q] = swapped[d].astype(jnp.bfloat16)
-
-    def far_copy(index):
+            if (q + 1) % per_step == 0:
+                send(q // per_step)
+
+    def far_copy(index, step):
         d = (nx - 1 - end) * owners + index
         return pltpu.make_async_remote_copy(
-            src_ref=tri_far.at[d],
-            dst_ref=tri_in.at[me],
-            send_sem=far_send.at[index],
-            recv_sem=tri_sems.at[1, lax.rem(d - me + plane, plane)],
+            src_ref=tri_far.at[d, pl.ds(step * per_step, per_step)],
+            dst_ref=tri_in.at[me, pl.ds(step * per_step, per_step)],
+            send_sem=far_send.at[step, index],
+            recv_sem=tri_sems.at[1, step, lax.rem(d - me + plane, plane)],
             device_id=(end, d // nz, lax.rem(d, nz)),
             device_id_type=MESH,
         )
 
-    def tri_copy(t):
+    def tri_copy(t, step):
         d, device = peer(t)
         return pltpu.make_async_remote_copy(
-            src_ref=tri_out.at[d],
-            dst_ref=tri_in.at[me],
-            send_sem=tri_sems.at[0, t],
-            recv_sem=tri_sems.at[1, t],
+            src_ref=tri_out.at[d, pl.ds(step * per_step, per_step)],
+            dst_ref=tri_in.at[me, pl.ds(step * per_step, per_step)],
+            send_sem=tri_sems.at[0, step, t],
+            recv_sem=tri_sems.at[1, step, t],
             device_id=device,
             device_id_type=MESH,
         )
 
+    def send_far(step):
+        for index in range(owners):
+            far_copy(index, step).start()
+
+    def send(step):
+        for t in range(1, plane):
+
+            @pl.when(jnp.logical_not(is_left_out(peer(t)[0])))
+            def _():
+                tri_copy(t, step).start()
+
+    def receive(step):
+        @pl.when(is_left_out(me))
+        def _():
+            tri_copy(0, step).wait_recv()
+
+        for t in range(1, plane):
+            tri_copy(t, step).wait_recv()
+
     @pl.when(is_helper)
     def _():
         left_copy.wait_recv()
-        multiply(left_far, tri_far)
-        for index in range(owners):
-            far_copy(index).start()
-
-    multiply(left_all, tri_out)
-    for t in range(1, plane):
-
-        @pl.when(jnp.logical_not(is_left_out(peer(t)[0])))
-        def _():
-            tri_copy(t).start()
+        multiply(left_far, tri_far, send_far)
+
+    multiply(left_all, tri_out, send)
 
     @pl.when(jnp.logical_not(is_left_out(me)))
     def _():
         tri_in[me] = tri_out[me]
-
-    @pl.when(is_left_out(me))
-    def _():
-        tri_copy(0).wait_recv()
-
-    for t in range(1, plane):
-        tri_copy(t).wait_recv()
 
     for load in loads[6:]:
         load.wait()
     for q in range(tiles):
+        if q % per_step == 0:
+            receive(q // per_step)
         lanes = slice(q * LANES, (q + 1) * LANES)
         sums = tri_in[:, q].reshape(hidden, LANES).astype(jnp.float32)
         centered = sums - jnp.mean(sums, axis=0, keepdims=True)
@@ -393,25 +427,27 @@
             (gating_ref[lanes, :] * mixed).astype(jnp.bfloat16).reshape(per_tile, width, channels)
         )
 
-    for copy in right_copies + left_copies:
+    for copy in sum(right_copies, left_copies):
         copy.wait_send()
     for t in range(1, plane):
 
         @pl.when(jnp.logical_not(is_left_out(peer(t)[0])))
         def _():
-            tri_copy(t).wait_send()
+            for step in range(TRI_STEPS):
+                tri_copy(t, step).wait_send()
 
     @pl.when(is_helper)
     def _():
         for index in range(owners):
-            far_copy(index).wait_send()
+            for step in range(TRI_STEPS):
+                far_copy(index, step).wait_send()
 
     @pl.when(is_end)
     def _():
         left_copy.wait_send()
 
     for t in range(nx - 2):
-        for piece in range(PIECES):
+        for piece in range(pieces):
             for way in range(2):
 
                 @pl.when(jnp.logical_and(has_ahead(way), has_origin(way, t)))
@@ -442,9 +478,9 @@
             pltpu.VMEM((rows * width, channels), jnp.bfloat16),
             pltpu.VMEM((rows * width, channels), jnp.float32),
         ]
-        + [pltpu.SemaphoreType.DMA((2, plane))] * 3
-        + [pltpu.SemaphoreType.DMA((2, nx - 2, PIECES))] * 2
-        + [pltpu.SemaphoreType.DMA((2,)), pltpu.SemaphoreType.DMA((rows // width,))]
+        + [pltpu.SemaphoreType.DMA((2, steps, plane)) for steps in (RIGHT_STEPS, 1, TRI_STEPS)]
+        + [pltpu.SemaphoreType.DMA((2, nx - 2, RIGHT_STEPS * PARTS))] * 2
+        + [pltpu.SemaphoreType.DMA((2,)), pltpu.SemaphoreType.DMA((TRI_STEPS, rows // width))]
         + [
             pltpu.VMEM(pair.shape, pair.dtype),
             pltpu.VMEM((width, rows), pair_mask.dtype),
@@ -483,6 +519,7 @@
             and rows * nx == LANES
             and rows % plane == 0
             and rows % width == 0
+            and rows * width % (RIGHT_STEPS * TRI_STEPS * LANES) == 0
             and nx >= 4
             and channels % LANES == 0
             and hidden % (16 * plane) == 0

time: 24.9 us -> 24.1 us (0.968)
  Pallas kernels: 23.2 us -> 22.4 us
    pallas_call x1, Pallas kernels: 23.2 us -> 22.4 us  [fused(): pl.pallas_call(functools.partial(kernel, nx, ny, nz), out_shape=jax.Shape...]
where the time goes in v4:
time: 24.1 us; the launch traced here: 24 us
  Pallas kernels  22.4 us (93%)
  local copies, waits for them, and re-layouts  1.57 us (7%)
    pallas_call x1, Pallas kernels, fused(): pl.pallas_call(functools.partial(kernel, nx, ny, nz), out_shape=jax.Shape...  22.4 us
    unnamed x1, local copies, waits for them, and re-layouts  1.57 us

profile of v4, /device:TPU:0, one launch (start us, length us, event | category | flops | bytes accessed | tf_op | source)
XLA Modules:
  0.0 24.0 jit_solution(1502020927091332494)
XLA Ops:
  0.0 22.4 %shard_map.91 = bf16[32,16,128]{2,1,0:T(8,128)(2,1)} custom-call(bf16[32,16,128]{2,1,0:T(8,128)(2,1)} %pair_hbm.1, s32[16,32]{1,0:T(8,128)} %bitcast.5, f32[1,128]{1,0:T(1,128)} %bitcast.6, f32[1,128]{1,0:T(1,128)} %bitcast.7, bf16[128,512]{1,0:T(8,128)(2,1)} %proj_hbm.1, bf16[128,128]{1,0:T(8,128)(2,1)} %gate_hbm.1, f32[1,128]{1,0:T(1,128)} %bitcast.8, ...), custom_call_target="tpu_custom_call" | custom-call | tf_op jit(solution)/shard_map/pallas_call | solution.py:466
  22.4 1.6 %copy.11 = bf16[32,16,128]{2,1,0:T(8,128)(2,1)} copy(bf16[32,16,128]{2,1,0:T(8,128)(2,1)} %shard_map.91) | data formatting | bytes 262144
